TPU v7x, 32 devices: a whole 2x2x4 slice. The times are simulated.
32 devices in a mesh: depth: 16 (over z, y, x), spec: 2 (over core).
Axes of the slice: x: 2, y: 2, z: 4, core: 2. Of those that a mesh axis runs over, the one named last changes fastest.
Arguments:
- emission: bfloat16 [512, 64, 2048], P('depth', 'spec'), may hold values from 0.099609375 to 2
- opacity: bfloat16 [512, 64, 2048], P('depth', 'spec'), may hold values from 0.29882812 to 3
- bin_extinction: float32 [64], P('spec'), may hold values from 0.1 to 30
- entry: int32 [2048], replicated, may hold values from 0 to 127
- exit_cell: int32 [2048], replicated, may hold values from 384 to 512
- response: float32 [3, 64], P(None, 'spec'), may hold values from 0.05 to 1
Outputs:
- nearer_slab_rgb: float32 [16, 3, 2048], P('depth')
- image: float32 [3, 2048], replicated
All inputs are finite; a program needn't handle non-finite values.
Results may differ from a plain program's by a relative error of at most 0.0003.
Values sent between devices are 32-bit elements; how exact they have to be, the bound alone decides.
A program may use at most 64 MiB of HBM per device.

v0:
```python
import functools
import math
import jax
import jax.numpy as jnp
from jax import lax
from jax.experimental import pallas as pl
from jax.experimental.pallas import tpu as pltpu
from jax.sharding import PartitionSpec as P

LANES = 128
MESH = pl.DeviceIdType.MESH


def column(row, eye):
    return jnp.sum(jnp.where(eye, row, 0.0), axis=1, keepdims=True)


def kernel(
    groups, members, specs,
    em_hbm, op_hbm, ext_ref, entry_ref, exit_ref, resp_ref,
    near_ref, image_ref,
    em_v, op_v, s_out, s_in, l_out, l_in, z_in, z_out, c_own, c_sib, t_out, t_in, f_out, f_in,
    r_out, r_in, i_out, i_in, front_v, whole_v,
    em_sem, op_sem, s_send, s_recv, l_send, l_recv, z_send, z_recv,
    c_send, c_recv, t_send, t_recv, f_send, f_recv, r_send, r_recv, i_send, i_recv,
):
    cells, bins, rays = em_hbm.shape
    part = rays // members
    tiles = part // LANES
    sections = groups * members
    cell_step = 1.0 / (cells * sections)
    me = lax.axis_index("depth")
    spec = lax.axis_index("spec")
    zi = me // members
    mi = me % members

    def owner(t):
        return lax.rem(mi + 1 + t, members)

    def rays_of(q):
        return pl.ds(pl.multiple_of(q * part, LANES), part)

    reads = []
    for hbm, vmem, sem in ((op_hbm, op_v, op_sem), (em_hbm, em_v, em_sem)):
        row = []
        for t in range(members):
            copy = pltpu.make_async_copy(hbm.at[:, :, rays_of(owner(t))], vmem.at[t], sem.at[t])
            copy.start()
            row.append(copy)
        reads.append(row)

    def peer_in_group(t):
        return (zi * members + owner(t), spec)

    outer = [(dz, ds) for dz in range(1, groups) for ds in range(specs)]

    def peer_outer(dz, ds):
        return (lax.rem(zi + dz, groups) * members + mi, lax.rem(spec + ds, specs))

    barrier = pltpu.get_barrier_semaphore()
    for t in range(members - 1):
        pl.semaphore_signal(barrier, inc=1, device_id=peer_in_group(t), device_id_type=MESH)
    for dz, ds in outer:
        pl.semaphore_signal(barrier, inc=1, device_id=peer_outer(dz, ds), device_id_type=MESH)
    for ds in range(1, specs):
        pl.semaphore_signal(
            barrier, inc=1, device_id=(me, lax.rem(spec + ds, specs)), device_id_type=MESH
        )

    eye = lax.broadcasted_iota(jnp.int32, (bins, bins), 0) == lax.broadcasted_iota(
        jnp.int32, (bins, bins), 1
    )
    scale = column(ext_ref[...].reshape(1, bins), eye) * (-cell_step * math.log2(math.e))
    scale = jnp.broadcast_to(scale, (bins, LANES))
    first = me * cells

    def bounds(q, j):
        at = pl.ds(pl.multiple_of(q * part + j * LANES, LANES), LANES)
        low = jnp.broadcast_to(entry_ref[at].reshape(1, LANES) - first, (8, LANES))
        high = jnp.broadcast_to(exit_ref[at].reshape(1, LANES) - first, (8, LANES))
        return low, high

    def live_at(i, low, high):
        return jnp.where((low <= i) & (high > i), 1.0, 0.0)

    def masked(x, live):
        return (x.astype(jnp.float32).reshape(bins // 8, 8, LANES) * live[None]).reshape(bins, LANES)

    def at_tile(j):
        return pl.ds(pl.multiple_of(j * LANES, LANES), LANES)

    sends = []
    for t in range(members):
        reads[0][t].wait()
        q = owner(t)

        @pl.loop(0, tiles)
        def _(j):
            low, high = bounds(q, j)
            total = jnp.zeros((bins, LANES), jnp.float32)
            for i in range(cells):
                total = total + masked(op_v[t, i, :, at_tile(j)], live_at(i, low, high))
            s_out[t, :, at_tile(j)] = total * scale

        if t == 0:
            pl.semaphore_wait(barrier, members - 1 + groups * specs - 1)
        if t < members - 1:
            copy = pltpu.make_async_remote_copy(
                s_out.at[t], s_in.at[mi], s_send.at[t], s_recv.at[mi],
                device_id=peer_in_group(t), device_id_type=MESH,
            )
            copy.start()
            sends.append(copy)

    for t in range(members):
        reads[1][t].wait()
        q = owner(t)

        @pl.loop(0, tiles)
        def _(j):
            low, high = bounds(q, j)
            run = jnp.zeros((bins, LANES), jnp.float32)
            glow = jnp.zeros((bins, LANES), jnp.float32)
            for i in range(cells):
                live = live_at(i, low, high)
                glow = glow + masked(em_v[t, i, :, at_tile(j)], live) * jnp.exp2(run)
                run = run + masked(op_v[t, i, :, at_tile(j)], live) * scale
            l_out[t, :, at_tile(j)] = glow * cell_step

        if t < members - 1:
            copy = pltpu.make_async_remote_copy(
                l_out.at[t], l_in.at[mi], l_send.at[t], l_recv.at[mi],
                device_id=peer_in_group(t), device_id_type=MESH,
            )
            copy.start()
            sends.append(copy)

    s_in[mi] = s_out[members - 1]
    l_in[mi] = l_out[members - 1]
    for t in range(members - 1):
        k = owner(t)
        pltpu.make_async_remote_copy(
            s_out.at[t], s_in.at[k], s_send.at[t], s_recv.at[k],
            device_id=peer_in_group(t), device_id_type=MESH,
        ).wait_recv()

    half = groups // 2

    def wait_light():
        for t in range(members - 1):
            k = owner(t)
            pltpu.make_async_remote_copy(
                l_out.at[t], l_in.at[k], l_send.at[t], l_recv.at[k],
                device_id=peer_in_group(t), device_id_type=MESH,
            ).wait_recv()

    def group_light(lanes):
        ahead = s_in[0, :, lanes]
        light = l_in[0, :, lanes]
        for k in range(1, members):
            light = light + jnp.exp2(ahead) * l_in[k, :, lanes]
            ahead = ahead + s_in[k, :, lanes]
        return light, ahead

    down = (lax.rem(zi + groups - 1, groups) * members + mi, spec)

    def down_copy(j):
        return pltpu.make_async_remote_copy(
            r_out.at[j], r_in.at[j], r_send.at[j], r_recv.at[j],
            device_id=down, device_id_type=MESH,
        )

    @pl.when(zi > half)
    def _():
        wait_light()
        for j in range(tiles):
            light, depth = group_light(pl.ds(j * LANES, LANES))
            r_out[j] = light

            @pl.when(zi < groups - 1)
            def _():
                down_copy(j).wait_recv()
                r_out[j] = light + jnp.exp2(depth) * r_in[j]

            down_copy(j).start()

    up = (lax.rem(zi + 1, groups) * members + mi, spec)

    def chain_copy(j):
        return pltpu.make_async_remote_copy(
            z_out.at[j], z_in.at[j], z_send.at[j], z_recv.at[j],
            device_id=up, device_id_type=MESH,
        )

    for j in range(tiles):
        lanes = pl.ds(j * LANES, LANES)
        here = s_in[0, :, lanes]
        for k in range(1, members):
            here = here + s_in[k, :, lanes]

        @pl.when(zi == 0)
        def _():
            z_in[j] = jnp.zeros((bins, LANES), jnp.float32)

        @pl.when(zi > 0)
        def _():
            chain_copy(j).wait_recv()

        @pl.when(zi < groups - 1)
        def _():
            z_out[j] = z_in[j] + here
            chain_copy(j).start()

    @pl.when(zi <= half)
    def _():
        wait_light()

    colours = resp_ref.shape[0]
    weights = [
        jnp.broadcast_to(column(resp_ref[pl.ds(c, 1), :], eye), (bins, LANES)) for c in range(colours)
    ]

    everyone = [(dz, ds) for dz in range(groups) for ds in range(specs) if dz + ds > 0]

    def image_copy(n, source):
        return pltpu.make_async_remote_copy(
            i_out, i_in.at[source], i_send.at[n], i_recv.at[source],
            device_id=peer_outer(*everyone[n]), device_id_type=MESH,
        )

    @pl.when(zi == half)
    def _():
        for j in range(tiles):
            lanes = pl.ds(j * LANES, LANES)
            light, depth = group_light(lanes)
            if half < groups - 1:
                down_copy(j).wait_recv()
                light = light + jnp.exp2(depth) * r_in[j]
            seen = jnp.exp2(z_in[j]) * light
            for c in range(colours):
                i_out[pl.ds(c, 1), lanes] = jnp.sum(seen * weights[c], axis=0, keepdims=True)
        for n in range(len(everyone)):
            image_copy(n, spec).start()
        i_in[spec] = i_out[...]

    for j in range(tiles):
        lanes = pl.ds(j * LANES, LANES)
        ahead = z_in[j]
        totals = [None] * colours
        for k in range(members):
            seen = jnp.exp2(ahead) * l_in[k, :, lanes]
            for c in range(colours):
                value = jnp.sum(seen * weights[c], axis=0, keepdims=True)
                c_own[k, pl.ds(c, 1), lanes] = value
                totals[c] = value if k == 0 else totals[c] + value
            if k < members - 1:
                ahead = ahead + s_in[k, :, lanes]
        for c in range(colours):
            t_out[pl.ds(c, 1), lanes] = totals[c]

    def total_copy(n, z, source):
        return pltpu.make_async_remote_copy(
            t_out, t_in.at[z, source], t_send.at[n], t_recv.at[z, source],
            device_id=peer_outer(*outer[n]), device_id_type=MESH,
        )

    def needed(origin, reader):
        return (origin < half) | (reader > origin)

    for n, (dz, ds) in enumerate(outer):
        @pl.when(needed(zi, lax.rem(zi + dz, groups)))
        def _():
            total_copy(n, zi, spec).start()

    for ds in range(1, specs):
        copy = pltpu.make_async_remote_copy(
            c_own, c_sib.at[spec], c_send.at[ds], c_recv.at[spec],
            device_id=(me, lax.rem(spec + ds, specs)), device_id_type=MESH,
        )
        copy.start()
        sends.append(copy)

    sums = [c_own[k] for k in range(members)]
    for ds in range(1, specs):
        other = lax.rem(spec + ds, specs)
        pltpu.make_async_remote_copy(
            c_own, c_sib.at[other], c_send.at[ds], c_recv.at[other],
            device_id=(me, other), device_id_type=MESH,
        ).wait_recv()
        sums = [sums[k] + c_sib[other, k] for k in range(members)]

    front_v[...] = jnp.zeros((colours, part), jnp.float32)
    whole = sums[0]
    for k in range(1, members):
        whole = whole + sums[k]
    whole_v[...] = whole * jnp.where(zi < half, 1.0, 0.0)
    for n, (dz, ds) in enumerate(outer):
        z = lax.rem(zi + dz, groups)
        other = lax.rem(spec + ds, specs)

        @pl.when(needed(z, zi))
        def _():
            total_copy(n, z, other).wait_recv()
            value = t_in[z, other]
            front_v[...] = front_v[...] + value * jnp.where(z < zi, 1.0, 0.0)
            whole_v[...] = whole_v[...] + value * jnp.where(z < half, 1.0, 0.0)

    front = front_v[...]
    whole = whole_v[...]
    for source in range(specs):
        @pl.when((zi != half) | (spec != source))
        def _():
            image_copy(0, source).wait_recv()

        whole = whole + i_in[source]

    for k in range(members):
        f_out[k, 0] = front
        f_out[k, 1] = whole
        if k < members - 1:
            front = front + sums[k]
    for t in range(members - 1):
        k = owner(t)
        copy = pltpu.make_async_remote_copy(
            f_out.at[k], f_in.at[mi], f_send.at[t], f_recv.at[mi],
            device_id=peer_in_group(t), device_id_type=MESH,
        )
        copy.start()
        sends.append(copy)
    near_ref[0, :, rays_of(mi)] = f_out[mi, 0]
    image_ref[:, rays_of(mi)] = f_out[mi, 1]
    for t in range(members - 1):
        k = owner(t)
        pltpu.make_async_remote_copy(
            f_out.at[k], f_in.at[k], f_send.at[t], f_recv.at[k],
            device_id=peer_in_group(t), device_id_type=MESH,
        ).wait_recv()
        near_ref[0, :, rays_of(k)] = f_in[k, 0]
        image_ref[:, rays_of(k)] = f_in[k, 1]

    for copy in sends:
        copy.wait_send()

    for n, (dz, ds) in enumerate(outer):
        @pl.when(needed(zi, lax.rem(zi + dz, groups)))
        def _():
            total_copy(n, zi, spec).wait_send()

    @pl.when(zi < groups - 1)
    def _():
        for j in range(tiles):
            chain_copy(j).wait_send()

    @pl.when(zi > half)
    def _():
        for j in range(tiles):
            down_copy(j).wait_send()

    @pl.when(zi == half)
    def _():
        for n in range(len(everyone)):
            image_copy(n, spec).wait_send()


def place(near_ref, image_ref, near_out, image_out):
    for c in range(near_out.shape[0]):
        near_out[c] = near_ref[:, c]
    image_out[...] = image_ref[...]


def body(groups, members, specs, emission, opacity, bin_extinction, entry, exit_cell, response):
    cells, bins, rays = emission.shape
    colours = response.shape[0]
    part = rays // members
    tiles = part // LANES
    f32 = jnp.float32
    vmem = pl.BlockSpec(memory_space=pltpu.VMEM)
    hbm = pl.BlockSpec(memory_space=pltpu.HBM)
    dma = pltpu.SemaphoreType.DMA
    near, image = pl.pallas_call(
        functools.partial(kernel, groups, members, specs),
        out_shape=(
            jax.ShapeDtypeStruct((1, colours, rays), f32),
            jax.ShapeDtypeStruct((colours, rays), f32),
        ),
        in_specs=[hbm, hbm, vmem, vmem, vmem, vmem],
        out_specs=(vmem, vmem),
        scratch_shapes=[
            pltpu.VMEM((members, cells, bins, part), emission.dtype),
            pltpu.VMEM((members, cells, bins, part), opacity.dtype),
            pltpu.VMEM((members, bins, part), f32),
            pltpu.VMEM((members, bins, part), f32),
            pltpu.VMEM((members, bins, part), f32),
            pltpu.VMEM((members, bins, part), f32),
            pltpu.VMEM((tiles, bins, LANES), f32),
            pltpu.VMEM((tiles, bins, LANES), f32),
            pltpu.VMEM((members, colours, part), f32),
            pltpu.VMEM((specs, members, colours, part), f32),
            pltpu.VMEM((colours, part), f32),
            pltpu.VMEM((groups, specs, colours, part), f32),
            pltpu.VMEM((members, 2, colours, part), f32),
            pltpu.VMEM((members, 2, colours, part), f32),
            pltpu.VMEM((tiles, bins, LANES), f32),
            pltpu.VMEM((tiles, bins, LANES), f32),
            pltpu.VMEM((colours, part), f32),
            pltpu.VMEM((specs, colours, part), f32),
            pltpu.VMEM((colours, part), f32),
            pltpu.VMEM((colours, part), f32),
            dma((members,)), dma((members,)),
            dma((members,)), dma((members,)),
            dma((members,)), dma((members,)),
            dma((tiles,)), dma((tiles,)),
            dma((specs,)), dma((specs,)),
            dma((groups * specs,)), dma((groups, specs)),
            dma((members,)), dma((members,)),
            dma((tiles,)), dma((tiles,)),
            dma((groups * specs,)), dma((specs,)),
        ],
        compiler_params=pltpu.CompilerParams(
            collective_id=0, has_side_effects=True, vmem_limit_bytes=56 * 2**20
        ),
    )(emission, opacity, bin_extinction, entry, exit_cell, response)
    near, image = pl.pallas_call(
        place,
        out_shape=(
            jax.ShapeDtypeStruct((colours, 1, rays), f32),
            jax.ShapeDtypeStruct((colours, rays), f32),
        ),
        in_specs=[vmem, vmem],
        out_specs=(vmem, vmem),
    )(near, image)
    return jnp.transpose(near, (1, 0, 2)), image


def solution(mesh):
    sections = mesh.shape["depth"]
    groups = next(g for g in range(1, sections + 1) if sections % g == 0 and g * g >= sections)
    placed = (
        P("depth", "spec", None),
        P("depth", "spec", None),
        P("spec"),
        P(),
        P(),
        P(None, "spec"),
    )
    return jax.shard_map(
        functools.partial(body, groups, sections // groups, mesh.shape["spec"]),
        mesh=mesh, in_specs=placed, out_specs=(P("depth", None, None), P()), check_vma=False,
    )
```

profile of v0, /device:TPU:0, one launch (start us, length us, event | category | flops | bytes accessed | tf_op | source)
XLA Modules:
  0.0 28.4 jit_solution(2675326564867511332)
XLA Ops:
  0.6 26.4 %shard_map.77 = (f32[1,3,2048]{2,1,0:T(4,128)}, f32[3,2048]{1,0:T(4,128)}) custom-call(bf16[32,32,2048]{2,1,0:T(8,128)(2,1)} %em_hbm.1, bf16[32,32,2048]{2,1,0:T(8,128)(2,1)} %op_hbm.1, f32[32]{0:T(128)} %ext_ref.1, s32[2048]{0:T(1024)} %entry_ref.1, s32[2048]{0:T(1024)} %exit_ref.1, f32[3,32]{1,0:T(4,128)} %resp_ref.1), custom_call_target="tpu_custom_call" | custom-call | tf_op jit(solution)/shard_map/pallas_call | solution.py:380
  27.0 1.4 %shard_map.78 = (f32[3,1,2048]{2,1,0:T(1,128)}, f32[3,2048]{1,0:T(4,128)}) custom-call(f32[1,3,2048]{2,1,0:T(4,128)} %get-tuple-element.6.near_ref, f32[3,2048]{1,0:T(4,128)} %get-tuple-element.7.image_ref), custom_call_target="tpu_custom_call" | custom-call | tf_op jit(solution)/shard_map/pallas_call | solution.py:423
where the time goes:
time: 28.6 us; the launch traced here: 28.4 us
  Pallas kernels  27.8 us (97%)
  between operations  0.64 us (2%)
    pallas_call x1, Pallas kernels, body(): pl.pallas_call(functools.partial(kernel, groups, members, specs), out_sha...  26.4 us
    pallas_call x1, Pallas kernels, body(): pl.pallas_call(place, out_shape=(jax.ShapeDtypeStruct((colours, 1, rays),...  1.4 us

commit v1 on v0

v1 whole, which is shorter than its diff:
```python
import functools
import math
import jax
import jax.numpy as jnp
from jax import lax
from jax.experimental import pallas as pl
from jax.experimental.pallas import tpu as pltpu
from jax.sharding import PartitionSpec as P

LANES = 128
SUBLANES = 8
MESH = pl.DeviceIdType.MESH


def padded(colours):
    return -(-colours // 4) * 4


def column(row, eye):
    return jnp.sum(jnp.where(eye, row, 0.0), axis=1, keepdims=True)


def kernel(
    groups, members, specs,
    em_hbm, op_hbm, ext_hbm, entry_hbm, exit_hbm, resp_hbm,
    near_ref, image_ref,
    em_v, op_v, ext_v, entry_v, exit_v, resp_v, w_own, w_all,
    s_out, s_in, l_out, l_in, d_out, d_in, f_out, f_in, x_out, x_in,
    em_sem, op_sem, small_sem, w_send, w_recv,
    s_send, s_recv, l_send, l_recv, d_send, d_recv, f_send, f_recv, x_send, x_recv, ready,
):
    cells, bins, rays = em_hbm.shape
    colours = resp_hbm.shape[0]
    tiles = rays // (members * LANES)
    half = rays // tiles
    rows = padded(colours)
    sections = groups * members
    cell_step = 1.0 / (cells * sections)
    me = lax.axis_index("depth")
    spec = lax.axis_index("spec")
    g = me // members
    mi = me % members
    lead = specs - 1
    is_lead = spec == lead
    last = members - 1
    paired = members & (members - 1) == 0

    def owner(t):
        if not paired:
            return (mi + 1 + t) % members
        if isinstance(t, int):
            mask = 0 if t == last else (t + 1) // 2 if t % 2 else last - t // 2
        else:
            odd = t % 2
            mask = jnp.where(t == last, 0, odd * ((t + 1) // 2) + (1 - odd) * (last - t // 2))
        who = 0
        bit = 1
        while bit < members:
            who = who + ((mi // bit + mask // bit) % 2) * bit
            bit *= 2
        return who

    def core(group, member, s):
        return (group * members + member, s)

    def read(hbm, vmem, sem, j):
        at = pl.ds(j * half, half)
        return pltpu.make_async_copy(hbm.at[:, :, at], vmem.at[:, :, at], sem.at[j])

    for j in range(tiles):
        read(op_hbm, op_v, op_sem, j).start()
    small = [
        pltpu.make_async_copy(hbm, vmem, small_sem.at[n])
        for n, (hbm, vmem) in enumerate(
            ((entry_hbm, entry_v), (exit_hbm, exit_v), (ext_hbm, ext_v), (resp_hbm, resp_v))
        )
    ]
    for copy in small:
        copy.start()

    barrier = pltpu.get_barrier_semaphore()
    near_barrier = groups == 2
    if near_barrier:
        other = 1 - g

        @pl.when(is_lead)
        def _():
            for t in range(members):
                for s in range(specs):
                    if t < last or s != lead:
                        pl.semaphore_signal(
                            barrier, inc=1, device_id=core(g, owner(t), s), device_id_type=MESH
                        )
            pl.semaphore_signal(barrier, inc=1, device_id=core(other, mi, lead), device_id_type=MESH)
    else:
        @pl.loop(1, sections * specs)
        def _(n):
            index = (me * specs + spec + n) % (sections * specs)
            pl.semaphore_signal(
                barrier, inc=1, device_id=(index // specs, index % specs), device_id_type=MESH
            )

    for j in range(tiles):
        read(em_hbm, em_v, em_sem, j).start()

    def enter():
        if near_barrier:
            @pl.when(is_lead)
            def _():
                pl.semaphore_wait(barrier, members)

            @pl.when(spec != lead)
            def _():
                pl.semaphore_wait(barrier, members)
        else:
            pl.semaphore_wait(barrier, sections * specs - 1)

    for copy in small:
        copy.wait()

    eye = lax.broadcasted_iota(jnp.int32, (bins, bins), 0) == lax.broadcasted_iota(
        jnp.int32, (bins, bins), 1
    )
    scale = column(ext_v[...].reshape(1, bins), eye) * (-cell_step * math.log2(math.e))
    scale = jnp.broadcast_to(scale, (bins, LANES))
    for c in range(colours):
        w_own[c] = jnp.broadcast_to(column(resp_v[pl.ds(c, 1), :], eye), (bins, LANES))
    x_out[...] = jnp.zeros_like(x_out)
    f_out[...] = jnp.zeros_like(f_out)
    first = me * cells

    def lanes(j, q):
        return pl.ds(pl.multiple_of((j * members + q) * LANES, LANES), LANES)

    def bounds(at):
        low = jnp.broadcast_to(entry_v[at].reshape(1, LANES) - first, (SUBLANES, LANES))
        high = jnp.broadcast_to(exit_v[at].reshape(1, LANES) - first, (SUBLANES, LANES))
        return low, high

    def live_at(i, low, high):
        return jnp.where((low <= i) & (high > i), 1.0, 0.0)

    def masked(x, live):
        x = x.astype(jnp.float32).reshape(bins // SUBLANES, SUBLANES, LANES)
        return (x * live[None]).reshape(bins, LANES)

    def depth_of(j, t):
        at = lanes(j, owner(t))
        low, high = bounds(at)
        total = jnp.zeros((bins, LANES), jnp.float32)
        for i in range(cells):
            total = total + masked(op_v[i, :, at], live_at(i, low, high))
        s_out[j, t] = total * scale

    def light_of(j, t):
        at = lanes(j, owner(t))
        low, high = bounds(at)
        run = jnp.zeros((bins, LANES), jnp.float32)
        glow = jnp.zeros((bins, LANES), jnp.float32)
        for i in range(cells):
            live = live_at(i, low, high)
            glow = glow + masked(em_v[i, :, at], live) * jnp.exp2(run)
            run = run + masked(op_v[i, :, at], live) * scale
        l_out[j, t] = glow * cell_step

    def piece(out, into, send, recv, j, t):
        return pltpu.make_async_remote_copy(
            out.at[j, t], into.at[j, mi, spec], send.at[j, t], recv.at[j, mi, spec],
            device_id=core(g, owner(t), lead), device_id_type=MESH,
        )

    def leaves(t):
        return (t < last) | (spec != lead)

    depth_args = (s_out, s_in, s_send, s_recv)
    light_args = (l_out, l_in, l_send, l_recv)

    def send(args, j, t):
        @pl.when(leaves(t))
        def _():
            piece(*args, j, t).start()

        @pl.when((t == last) & is_lead)
        def _():
            args[1][j, mi, spec] = args[0][j, t]

    w_copies = [
        pltpu.make_async_remote_copy(
            w_own, w_all.at[spec], w_send, w_recv.at[spec],
            device_id=(me, lead), device_id_type=MESH,
        )
    ]

    for j in range(tiles):
        read(op_hbm, op_v, op_sem, j).wait()
        if j == 0:
            @pl.loop(0, members)
            def _(t):
                depth_of(0, t)

            enter()

            @pl.loop(0, members)
            def _(t):
                send(depth_args, 0, t)
        else:
            @pl.loop(0, members)
            def _(t):
                depth_of(j, t)
                send(depth_args, j, t)

    @pl.when(is_lead)
    def _():
        w_all[lead] = w_own[...]

    @pl.when(spec != lead)
    def _():
        w_copies[0].start()

    for j in range(tiles):
        read(em_hbm, em_v, em_sem, j).wait()

        @pl.loop(0, members)
        def _(t):
            light_of(j, t)
            send(light_args, j, t)

    def arrive(args, j):
        out, into, send_sem, recv_sem = args
        for t in range(members):
            for s in range(specs):
                if t < last or s != lead:
                    k = owner(t)
                    pltpu.make_async_remote_copy(
                        out.at[j, t], into.at[j, k, s], send_sem.at[j, t], recv_sem.at[j, k, s],
                        device_id=core(g, k, s), device_id_type=MESH,
                    ).wait_recv()

    def chain(j):
        return pltpu.make_async_remote_copy(
            d_out.at[j], d_in.at[j], d_send.at[j], d_recv.at[j],
            device_id=core((g + 1) % groups, mi, lead), device_id_type=MESH,
        )

    def total_copy(dg, t, s):
        return pltpu.make_async_remote_copy(
            x_out, x_in.at[g, mi], x_send.at[dg - 1, t, s], x_recv.at[g, mi],
            device_id=core((g + dg) % groups, owner(t), s), device_id_type=MESH,
        )

    def block_copy(t, s):
        k = owner(t)
        return pltpu.make_async_remote_copy(
            f_out.at[k], f_in.at[mi], f_send.at[t, s], f_recv.at[mi],
            device_id=core(g, k, s), device_id_type=MESH,
        )

    @pl.when(is_lead)
    def _():
        for j in range(tiles):
            arrive(depth_args, j)

            @pl.when(g == 0)
            def _():
                d_in[j] = jnp.zeros(d_in.shape[1:], jnp.float32)

            if groups > 1:
                @pl.when(g < groups - 1)
                def _():
                    here = s_in[j, 0]
                    for k in range(1, members):
                        here = here + s_in[j, k]
                    if groups > 2:
                        @pl.when(g > 0)
                        def _():
                            chain(j).wait_recv()

                        here = here + d_in[j]
                    d_out[j] = here
                    chain(j).start()

        if near_barrier:
            @pl.when(g == 1)
            def _():
                pl.semaphore_signal(ready, inc=1, device_id=core(0, mi, lead), device_id_type=MESH)

        for s in range(specs):
            if s != lead:
                pltpu.make_async_remote_copy(
                    w_own, w_all.at[s], w_send, w_recv.at[s], device_id=(me, s), device_id_type=MESH,
                ).wait_recv()

        for j in range(tiles):
            arrive(light_args, j)
            if groups > 1:
                @pl.when((g > 0) if groups == 2 else (g == groups - 1))
                def _():
                    chain(j).wait_recv()

            ahead = d_in[j]
            sums = [jnp.zeros((SUBLANES, LANES), jnp.float32) for _ in range(colours)]
            for k in range(members):
                seen = jnp.exp2(ahead) * l_in[j, k]
                for c in range(colours):
                    if k > 0:
                        f_out[k, 0, pl.ds(rows * j + c, 1), :] = jnp.sum(sums[c], axis=0, keepdims=True)
                    part = (seen * w_all[:, c]).reshape(-1, SUBLANES, LANES)
                    sums[c] = sums[c] + jnp.sum(part, axis=0)
                if k < members - 1:
                    ahead = ahead + s_in[j, k]
            for c in range(colours):
                x_out[pl.ds(rows * j + c, 1), :] = jnp.sum(sums[c], axis=0, keepdims=True)

        if near_barrier:
            @pl.when(g == 0)
            def _():
                pl.semaphore_wait(ready, 1)

        for dg in range(1, groups):
            for t in range(members):
                for s in range(specs):
                    total_copy(dg, t, s).start()
        for k in range(members):
            f_out[k, 1] = x_out[...]
        for t in range(members):
            for s in range(specs):
                if t < last or s != lead:
                    block_copy(t, s).start()
        f_in[mi] = f_out[mi]

    for t in range(members):
        q = owner(t)

        @pl.when(leaves(t))
        def _():
            pltpu.make_async_remote_copy(
                f_out.at[0], f_in.at[q], f_send.at[t, 0], f_recv.at[q],
                device_id=core(g, q, lead), device_id_type=MESH,
            ).wait_recv()

    for dg in range(1, groups):
        src = (g + dg) % groups
        for q in range(members):
            pltpu.make_async_remote_copy(
                x_out, x_in.at[src, q], x_send.at[0, 0, 0], x_recv.at[src, q],
                device_id=core(src, q, lead), device_id_type=MESH,
            ).wait_recv()

    for q in range(members):
        near = f_in[q, 0]
        image = f_in[q, 1]
        for dg in range(1, groups):
            src = (g + dg) % groups
            value = x_in[src, q]
            near = near + value * jnp.where(src < g, 1.0, 0.0)
            image = image + value
        for j in range(tiles):
            at = pl.ds((j * members + q) * LANES, LANES)
            near_ref[0, :, at] = near[4 * j:rows * j + colours]
            image_ref[:, at] = image[4 * j:rows * j + colours]

    for args in (depth_args, light_args):
        for j in range(tiles):
            @pl.loop(0, members)
            def _(t):
                @pl.when(leaves(t))
                def _():
                    piece(*args, j, t).wait_send()

    @pl.when(spec != lead)
    def _():
        w_copies[0].wait_send()

    @pl.when(is_lead)
    def _():
        for j in range(tiles):
            if groups > 1:
                @pl.when(g < groups - 1)
                def _():
                    chain(j).wait_send()
        for t in range(members):
            for s in range(specs):
                for dg in range(1, groups):
                    total_copy(dg, t, s).wait_send()
                if t < last or s != lead:
                    block_copy(t, s).wait_send()


def place(near_ref, image_ref, near_out, image_out):
    for c in range(near_out.shape[0]):
        near_out[c] = near_ref[:, c]
    image_out[...] = image_ref[...]


def body(groups, members, specs, emission, opacity, bin_extinction, entry, exit_cell, response):
    cells, bins, rays = emission.shape
    colours = response.shape[0]
    tiles = rays // (members * LANES)
    rows = padded(colours)
    f32 = jnp.float32
    vmem = pl.BlockSpec(memory_space=pltpu.VMEM)
    hbm = pl.BlockSpec(memory_space=pltpu.HBM)
    dma = pltpu.SemaphoreType.DMA
    near, image = pl.pallas_call(
        functools.partial(kernel, groups, members, specs),
        out_shape=(
            jax.ShapeDtypeStruct((1, colours, rays), f32),
            jax.ShapeDtypeStruct((colours, rays), f32),
        ),
        in_specs=[hbm] * 6,
        out_specs=(vmem, vmem),
        scratch_shapes=[
            pltpu.VMEM(emission.shape, emission.dtype),
            pltpu.VMEM(opacity.shape, opacity.dtype),
            pltpu.VMEM((bins,), f32),
            pltpu.VMEM((rays,), jnp.int32),
            pltpu.VMEM((rays,), jnp.int32),
            pltpu.VMEM((colours, bins), f32),
            pltpu.VMEM((colours, bins, LANES), f32),
            pltpu.VMEM((specs, colours, bins, LANES), f32),
            pltpu.VMEM((tiles, members, bins, LANES), f32),
            pltpu.VMEM((tiles, members, specs, bins, LANES), f32),
            pltpu.VMEM((tiles, members, bins, LANES), f32),
            pltpu.VMEM((tiles, members, specs, bins, LANES), f32),
            pltpu.VMEM((tiles, specs, bins, LANES), f32),
            pltpu.VMEM((tiles, specs, bins, LANES), f32),
            pltpu.VMEM((members, 2, rows * tiles, LANES), f32),
            pltpu.VMEM((members, 2, rows * tiles, LANES), f32),
            pltpu.VMEM((rows * tiles, LANES), f32),
            pltpu.VMEM((groups, members, rows * tiles, LANES), f32),
            dma((tiles,)), dma((tiles,)), dma((4,)), dma, dma((specs,)),
            dma((tiles, members)), dma((tiles, members, specs)),
            dma((tiles, members)), dma((tiles, members, specs)),
            dma((tiles,)), dma((tiles,)),
            dma((members, specs)), dma((members,)),
            dma((max(groups - 1, 1), members, specs)), dma((groups, members)),
            pltpu.SemaphoreType.REGULAR,
        ],
        compiler_params=pltpu.CompilerParams(
            collective_id=0, has_side_effects=True, vmem_limit_bytes=56 * 2**20
        ),
    )(emission, opacity, bin_extinction, entry, exit_cell, response)
    near, image = pl.pallas_call(
        place,
        out_shape=(
            jax.ShapeDtypeStruct((colours, 1, rays), f32),
            jax.ShapeDtypeStruct((colours, rays), f32),
        ),
        in_specs=[vmem, vmem],
        out_specs=(vmem, vmem),
    )(near, image)
    return jnp.transpose(near, (1, 0, 2)), image


def solution(mesh):
    sections = mesh.shape["depth"]
    specs = mesh.shape["spec"]

    def program(emission, *rest):
        rays = emission.shape[2]
        members = max(
            m for m in range(1, sections + 1)
            if sections % m == 0 and rays % (m * LANES) == 0 and (2 * m <= sections or m == 1)
        )
        placed = (
            P("depth", "spec", None),
            P("depth", "spec", None),
            P("spec"),
            P(),
            P(),
            P(None, "spec"),
        )
        return jax.shard_map(
            functools.partial(body, sections // members, members, specs),
            mesh=mesh, in_specs=placed, out_specs=(P("depth", None, None), P()), check_vma=False,
        )(emission, *rest)

    return program
```

time: 28.6 us -> 23.1 us (0.81)
  Pallas kernels: 27.8 us -> 22.3 us
    pallas_call x1, Pallas kernels: 26.4 us -> 20.9 us  [body(): pl.pallas_call(functools.partial(kernel, groups, members, specs), out_sha...]
where the time goes in v1:
time: 23.1 us; the launch traced here: 22.9 us
  Pallas kernels  22.3 us (97%)
  between operations  0.64 us (3%)
    pallas_call x1, Pallas kernels, body(): pl.pallas_call(functools.partial(kernel, groups, members, specs), out_sha...  20.9 us
    pallas_call x1, Pallas kernels, body(): pl.pallas_call(place, out_shape=(jax.ShapeDtypeStruct((colours, 1, rays),...  1.4 us

profile of v1, /device:TPU:0, one launch (start us, length us, event | category | flops | bytes accessed | tf_op | source)
XLA Modules:
  0.0 22.9 jit_solution(4619257244977069655)
XLA Ops:
  0.6 20.9 %shard_map.77 = (f32[1,3,2048]{2,1,0:T(4,128)}, f32[3,2048]{1,0:T(4,128)}) custom-call(bf16[32,32,2048]{2,1,0:T(8,128)(2,1)} %em_hbm.1, bf16[32,32,2048]{2,1,0:T(8,128)(2,1)} %op_hbm.1, f32[32]{0:T(128)} %ext_hbm.1, s32[2048]{0:T(1024)} %entry_hbm.1, s32[2048]{0:T(1024)} %exit_hbm.1, f32[3,32]{1,0:T(4,128)} %resp_hbm.1), custom_call_target="tpu_custom_call" | custom-call | tf_op jit(solution)/shard_map/pallas_call | solution.py:404
  21.5 1.4 %shard_map.78 = (f32[3,1,2048]{2,1,0:T(1,128)}, f32[3,2048]{1,0:T(4,128)}) custom-call(f32[1,3,2048]{2,1,0:T(4,128)} %get-tuple-element.6.near_ref, f32[3,2048]{1,0:T(4,128)} %get-tuple-element.7.image_ref), custom_call_target="tpu_custom_call" | custom-call | tf_op jit(solution)/shard_map/pallas_call | solution.py:443

commit v2 on v1

--- a/solution.py
+++ b/solution.py
@@ -26,7 +26,7 @@
     near_ref, image_ref,
     em_v, op_v, ext_v, entry_v, exit_v, resp_v, w_own, w_all,
     s_out, s_in, l_out, l_in, d_out, d_in, f_out, f_in, x_out, x_in,
-    em_sem, op_sem, small_sem, w_send, w_recv,
+    em_sem, op_sem, piece_sem, small_sem, w_send, w_recv,
     s_send, s_recv, l_send, l_recv, d_send, d_recv, f_send, f_recv, x_send, x_recv, ready,
 ):
     cells, bins, rays = em_hbm.shape
@@ -63,12 +63,9 @@
     def core(group, member, s):
         return (group * members + member, s)
 
-    def read(hbm, vmem, sem, j):
-        at = pl.ds(j * half, half)
-        return pltpu.make_async_copy(hbm.at[:, :, at], vmem.at[:, :, at], sem.at[j])
-
-    for j in range(tiles):
-        read(op_hbm, op_v, op_sem, j).start()
+    def lanes(j, q):
+        return pl.ds(pl.multiple_of((j * members + q) * LANES, LANES), LANES)
+
     small = [
         pltpu.make_async_copy(hbm, vmem, small_sem.at[n])
         for n, (hbm, vmem) in enumerate(
@@ -77,6 +74,19 @@
     ]
     for copy in small:
         copy.start()
+
+    def read_piece(t):
+        at = lanes(0, owner(t))
+        return pltpu.make_async_copy(op_hbm.at[:, :, at], op_v.at[:, :, at], piece_sem.at[t])
+
+    def read(hbm, vmem, sem, j):
+        at = pl.ds(j * half, half)
+        return pltpu.make_async_copy(hbm.at[:, :, at], vmem.at[:, :, at], sem.at[j])
+
+    for t in range(members):
+        read_piece(t).start()
+    for j in range(1, tiles):
+        read(op_hbm, op_v, op_sem, j).start()
 
     barrier = pltpu.get_barrier_semaphore()
     near_barrier = groups == 2
@@ -129,9 +139,6 @@
     f_out[...] = jnp.zeros_like(f_out)
     first = me * cells
 
-    def lanes(j, q):
-        return pl.ds(pl.multiple_of((j * members + q) * LANES, LANES), LANES)
-
     def bounds(at):
         low = jnp.broadcast_to(entry_v[at].reshape(1, LANES) - first, (SUBLANES, LANES))
         high = jnp.broadcast_to(exit_v[at].reshape(1, LANES) - first, (SUBLANES, LANES))
@@ -165,7 +172,7 @@
 
     def piece(out, into, send, recv, j, t):
         return pltpu.make_async_remote_copy(
-            out.at[j, t], into.at[j, mi, spec], send.at[j, t], recv.at[j, mi, spec],
+            out.at[j, t], into.at[j, mi * specs + spec], send, recv.at[j],
             device_id=core(g, owner(t), lead), device_id_type=MESH,
         )
 
@@ -182,32 +189,26 @@
 
         @pl.when((t == last) & is_lead)
         def _():
-            args[1][j, mi, spec] = args[0][j, t]
-
-    w_copies = [
-        pltpu.make_async_remote_copy(
-            w_own, w_all.at[spec], w_send, w_recv.at[spec],
-            device_id=(me, lead), device_id_type=MESH,
-        )
-    ]
+            args[1][j, mi * specs + spec] = args[0][j, t]
+
+    weights_copy = pltpu.make_async_remote_copy(
+        w_own, w_all.at[spec], w_send, w_recv, device_id=(me, lead), device_id_type=MESH,
+    )
 
     for j in range(tiles):
-        read(op_hbm, op_v, op_sem, j).wait()
-        if j == 0:
-            @pl.loop(0, members)
-            def _(t):
-                depth_of(0, t)
-
-            enter()
-
-            @pl.loop(0, members)
-            def _(t):
-                send(depth_args, 0, t)
-        else:
-            @pl.loop(0, members)
-            def _(t):
-                depth_of(j, t)
-                send(depth_args, j, t)
+        if j > 0:
+            read(op_hbm, op_v, op_sem, j).wait()
+
+        @pl.loop(0, members)
+        def _(t):
+            if j == 0:
+                read_piece(t).wait()
+            depth_of(j, t)
+            if j == 0:
+                @pl.when(t == 0)
+                def _():
+                    enter()
+            send(depth_args, j, t)
 
     @pl.when(is_lead)
     def _():
@@ -215,7 +216,7 @@
 
     @pl.when(spec != lead)
     def _():
-        w_copies[0].start()
+        weights_copy.start()
 
     for j in range(tiles):
         read(em_hbm, em_v, em_sem, j).wait()
@@ -225,33 +226,38 @@
             light_of(j, t)
             send(light_args, j, t)
 
+    def landed(ref, recv):
+        pltpu.make_async_remote_copy(
+            ref, ref, w_send, recv, device_id=(me, lead), device_id_type=MESH
+        ).wait_recv()
+
+    def drained(ref, send):
+        pltpu.make_async_remote_copy(
+            ref, ref, send, w_recv, device_id=(me, lead), device_id_type=MESH
+        ).wait_send()
+
     def arrive(args, j):
-        out, into, send_sem, recv_sem = args
-        for t in range(members):
-            for s in range(specs):
-                if t < last or s != lead:
-                    k = owner(t)
-                    pltpu.make_async_remote_copy(
-                        out.at[j, t], into.at[j, k, s], send_sem.at[j, t], recv_sem.at[j, k, s],
-                        device_id=core(g, k, s), device_id_type=MESH,
-                    ).wait_recv()
+        landed(args[1].at[j, pl.ds(0, members * specs - 1)], args[3].at[j])
+
+    def section(ref, j, k):
+        return ref[j, pl.ds(k * specs, specs)]
 
     def chain(j):
         return pltpu.make_async_remote_copy(
-            d_out.at[j], d_in.at[j], d_send.at[j], d_recv.at[j],
+            d_out.at[j], d_in.at[j], d_send, d_recv.at[j],
             device_id=core((g + 1) % groups, mi, lead), device_id_type=MESH,
         )
 
     def total_copy(dg, t, s):
         return pltpu.make_async_remote_copy(
-            x_out, x_in.at[g, mi], x_send.at[dg - 1, t, s], x_recv.at[g, mi],
+            x_out, x_in.at[dg - 1, mi], x_send.at[dg - 1, s], x_recv.at[dg - 1],
             device_id=core((g + dg) % groups, owner(t), s), device_id_type=MESH,
         )
 
     def block_copy(t, s):
         k = owner(t)
         return pltpu.make_async_remote_copy(
-            f_out.at[k], f_in.at[mi], f_send.at[t, s], f_recv.at[mi],
+            f_out.at[k], f_in.at[mi], f_send.at[s], f_recv,
             device_id=core(g, k, s), device_id_type=MESH,
         )
 
@@ -267,9 +273,9 @@
             if groups > 1:
                 @pl.when(g < groups - 1)
                 def _():
-                    here = s_in[j, 0]
+                    here = section(s_in, j, 0)
                     for k in range(1, members):
-                        here = here + s_in[j, k]
+                        here = here + section(s_in, j, k)
                     if groups > 2:
                         @pl.when(g > 0)
                         def _():
@@ -284,11 +290,8 @@
             def _():
                 pl.semaphore_signal(ready, inc=1, device_id=core(0, mi, lead), device_id_type=MESH)
 
-        for s in range(specs):
-            if s != lead:
-                pltpu.make_async_remote_copy(
-                    w_own, w_all.at[s], w_send, w_recv.at[s], device_id=(me, s), device_id_type=MESH,
-                ).wait_recv()
+        if specs > 1:
+            landed(w_all.at[pl.ds(0, specs - 1)], w_recv)
 
         for j in range(tiles):
             arrive(light_args, j)
@@ -300,14 +303,14 @@
             ahead = d_in[j]
             sums = [jnp.zeros((SUBLANES, LANES), jnp.float32) for _ in range(colours)]
             for k in range(members):
-                seen = jnp.exp2(ahead) * l_in[j, k]
+                seen = jnp.exp2(ahead) * section(l_in, j, k)
                 for c in range(colours):
                     if k > 0:
                         f_out[k, 0, pl.ds(rows * j + c, 1), :] = jnp.sum(sums[c], axis=0, keepdims=True)
                     part = (seen * w_all[:, c]).reshape(-1, SUBLANES, LANES)
                     sums[c] = sums[c] + jnp.sum(part, axis=0)
                 if k < members - 1:
-                    ahead = ahead + s_in[j, k]
+                    ahead = ahead + section(s_in, j, k)
             for c in range(colours):
                 x_out[pl.ds(rows * j + c, 1), :] = jnp.sum(sums[c], axis=0, keepdims=True)
 
@@ -328,62 +331,48 @@
                     block_copy(t, s).start()
         f_in[mi] = f_out[mi]
 
-    for t in range(members):
-        q = owner(t)
-
-        @pl.when(leaves(t))
-        def _():
-            pltpu.make_async_remote_copy(
-                f_out.at[0], f_in.at[q], f_send.at[t, 0], f_recv.at[q],
-                device_id=core(g, q, lead), device_id_type=MESH,
-            ).wait_recv()
+    @pl.when(is_lead)
+    def _():
+        landed(f_in.at[pl.ds(0, last)], f_recv)
+
+    @pl.when(spec != lead)
+    def _():
+        landed(f_in, f_recv)
 
     for dg in range(1, groups):
-        src = (g + dg) % groups
-        for q in range(members):
-            pltpu.make_async_remote_copy(
-                x_out, x_in.at[src, q], x_send.at[0, 0, 0], x_recv.at[src, q],
-                device_id=core(src, q, lead), device_id_type=MESH,
-            ).wait_recv()
+        landed(x_in.at[dg - 1], x_recv.at[dg - 1])
 
     for q in range(members):
         near = f_in[q, 0]
         image = f_in[q, 1]
         for dg in range(1, groups):
-            src = (g + dg) % groups
-            value = x_in[src, q]
+            src = (g + groups - dg) % groups
+            value = x_in[dg - 1, q]
             near = near + value * jnp.where(src < g, 1.0, 0.0)
             image = image + value
         for j in range(tiles):
             at = pl.ds((j * members + q) * LANES, LANES)
             near_ref[0, :, at] = near[4 * j:rows * j + colours]
             image_ref[:, at] = image[4 * j:rows * j + colours]
-
-    for args in (depth_args, light_args):
-        for j in range(tiles):
-            @pl.loop(0, members)
-            def _(t):
-                @pl.when(leaves(t))
-                def _():
-                    piece(*args, j, t).wait_send()
+    @pl.when(is_lead)
+    def _():
+        drained(s_out.at[:, pl.ds(0, last)], s_send)
+        drained(l_out.at[:, pl.ds(0, last)], l_send)
+        if groups > 1:
+            @pl.when(g < groups - 1)
+            def _():
+                drained(d_out, d_send)
+        for s in range(specs):
+            drained(f_out.at[pl.ds(0, members if s != lead else last)], f_send.at[s])
+        for dg in range(1, groups):
+            for s in range(specs):
+                drained(x_in.at[dg - 1], x_send.at[dg - 1, s])
 
     @pl.when(spec != lead)
     def _():
-        w_copies[0].wait_send()
-
-    @pl.when(is_lead)
-    def _():
-        for j in range(tiles):
-            if groups > 1:
-                @pl.when(g < groups - 1)
-                def _():
-                    chain(j).wait_send()
-        for t in range(members):
-            for s in range(specs):
-                for dg in range(1, groups):
-                    total_copy(dg, t, s).wait_send()
-                if t < last or s != lead:
-                    block_copy(t, s).wait_send()
+        drained(s_out, s_send)
+        drained(l_out, l_send)
+        weights_copy.wait_send()
 
 
 def place(near_ref, image_ref, near_out, image_out):
@@ -404,8 +393,8 @@
     near, image = pl.pallas_call(
         functools.partial(kernel, groups, members, specs),
         out_shape=(
-            jax.ShapeDtypeStruct((1, colours, rays), f32),
-            jax.ShapeDtypeStruct((colours, rays), f32),
+            pltpu.VMEM((1, colours, rays), f32),
+            pltpu.VMEM((colours, rays), f32),
         ),
         in_specs=[hbm] * 6,
         out_specs=(vmem, vmem),
@@ -419,21 +408,18 @@
             pltpu.VMEM((colours, bins, LANES), f32),
             pltpu.VMEM((specs, colours, bins, LANES), f32),
             pltpu.VMEM((tiles, members, bins, LANES), f32),
-            pltpu.VMEM((tiles, members, specs, bins, LANES), f32),
+            pltpu.VMEM((tiles, members * specs, bins, LANES), f32),
             pltpu.VMEM((tiles, members, bins, LANES), f32),
-            pltpu.VMEM((tiles, members, specs, bins, LANES), f32),
+            pltpu.VMEM((tiles, members * specs, bins, LANES), f32),
             pltpu.VMEM((tiles, specs, bins, LANES), f32),
             pltpu.VMEM((tiles, specs, bins, LANES), f32),
             pltpu.VMEM((members, 2, rows * tiles, LANES), f32),
             pltpu.VMEM((members, 2, rows * tiles, LANES), f32),
             pltpu.VMEM((rows * tiles, LANES), f32),
-            pltpu.VMEM((groups, members, rows * tiles, LANES), f32),
-            dma((tiles,)), dma((tiles,)), dma((4,)), dma, dma((specs,)),
-            dma((tiles, members)), dma((tiles, members, specs)),
-            dma((tiles, members)), dma((tiles, members, specs)),
-            dma((tiles,)), dma((tiles,)),
-            dma((members, specs)), dma((members,)),
-            dma((max(groups - 1, 1), members, specs)), dma((groups, members)),
+            pltpu.VMEM((max(groups - 1, 1), members, rows * tiles, LANES), f32),
+            dma((tiles,)), dma((tiles,)), dma((members,)), dma((4,)), dma, dma,
+            dma, dma((tiles,)), dma, dma((tiles,)), dma, dma((tiles,)),
+            dma((specs,)), dma, dma((max(groups - 1, 1), specs)), dma((max(groups - 1, 1),)),
             pltpu.SemaphoreType.REGULAR,
         ],
         compiler_params=pltpu.CompilerParams(
@@ -448,7 +434,7 @@
         ),
         in_specs=[vmem, vmem],
         out_specs=(vmem, vmem),
-    )(near, image)
+    )(*(pltpu.with_memory_space_constraint(x, pltpu.VMEM) for x in (near, image)))
     return jnp.transpose(near, (1, 0, 2)), image
 
 

time: 23.1 us -> 20.1 us (0.87)
  Pallas kernels: 22.3 us -> 19.3 us
    pallas_call x1, Pallas kernels: 20.9 us -> 18.7 us  [body(): pl.pallas_call(functools.partial(kernel, groups, members, specs), out_sha...]
    pallas_call x1, Pallas kernels: 1.4 us -> 0.63 us  [body(): pl.pallas_call(place, out_shape=(jax.ShapeDtypeStruct((colours, 1, rays),...]
where the time goes in v2:
time: 20.1 us; the launch traced here: 19.9 us
  Pallas kernels  19.3 us (96%)
  between operations  0.64 us (3%)
    pallas_call x1, Pallas kernels, body(): pl.pallas_call(functools.partial(kernel, groups, members, specs), out_sha...  18.7 us
    pallas_call x1, Pallas kernels, body(): pl.pallas_call(place, out_shape=(jax.ShapeDtypeStruct((colours, 1, rays),...  0.63 us

profile of v2, /device:TPU:0, one launch (start us, length us, event | category | flops | bytes accessed | tf_op | source)
XLA Modules:
  0.0 19.9 jit_solution(11366190116821420599)
XLA Ops:
  0.6 18.7 %shard_map.77 = (f32[1,3,2048]{2,1,0:T(4,128)S(1)}, f32[3,2048]{1,0:T(4,128)S(1)}) custom-call(bf16[32,32,2048]{2,1,0:T(8,128)(2,1)} %em_hbm.1, bf16[32,32,2048]{2,1,0:T(8,128)(2,1)} %op_hbm.1, f32[32]{0:T(128)} %ext_hbm.1, s32[2048]{0:T(1024)} %entry_hbm.1, s32[2048]{0:T(1024)} %exit_hbm.1, f32[3,32]{1,0:T(4,128)} %resp_hbm.1), custom_call_target="tpu_custom_call" | custom-call | tf_op jit(solution)/shard_map/pallas_call | solution.py:393
  19.3 0.6 %shard_map.78 = (f32[3,1,2048]{2,1,0:T(1,128)}, f32[3,2048]{1,0:T(4,128)}) custom-call(f32[1,3,2048]{2,1,0:T(4,128)S(1)} %get-tuple-element.6.near_ref, f32[3,2048]{1,0:T(4,128)S(1)} %get-tuple-element.7.image_ref), custom_call_target="tpu_custom_call" | custom-call | tf_op jit(solution)/shard_map/pallas_call | solution.py:429
